TPU v7x, 32 devices: a whole 2x2x4 slice. The times are simulated.
32 devices in a mesh: image: 2 (over y), ga: 4 (over z), band: 4 (over x, core).
Axes of the slice: x: 2, y: 2, z: 4, core: 2. Of those that a mesh axis runs over, the one named last changes fastest.
Arguments:
- projectors: bfloat16 [160, 655360], P(('image', 'band'), 'ga'), parts along dimension 0, may hold values from -6 to 6
- occupied: bfloat16 [256, 655360], P(('image', 'band'), 'ga'), parts along dimension 0, may hold values from -0.0009765625 to 0.0009765625
- block: bfloat16 [512, 655360], P(('image', 'band'), 'ga'), parts along dimension 0, may hold values from -0.0078125 to 0.0078125
- weights: float32 [256], P(('image', 'band')), parts along dimension 0, may hold values from 0.1 to 1
- u_index: int32 [16], replicated, may hold values from 0 to 3
- u_values: float32 [4], replicated, may hold values from 0.5 to 2
Outputs:
- applied: bfloat16 [512, 655360], P(('image', 'band'), 'ga'), parts along dimension 0
There are 2 independent parts, one for each index of `image`. A program takes and returns all parts, laid end to end along the dimension named above; an argument that names none is the same for every part. Nothing has to cross between parts.
Inputs may be any that keep to these rules, and one draw needn't show every extreme that they name: `u_index`: each atom's entry of the U table.
All inputs are finite; a program needn't handle non-finite values.
Results may differ from a plain program's by a relative error of at most 0.0049.
Values may be sent and summed in bfloat16 or wider, within the bound.
A program may use at most 192 MiB of HBM per device.

v0:
```python
import functools
import math

import jax
import jax.numpy as jnp
from jax import lax
from jax.experimental import pallas as pl
from jax.experimental.pallas import tpu as pltpu
from jax.sharding import PartitionSpec as P

ORB = 5
LANES = 128
SUBLANES = 8
CORES = 2
STEPS = 16
BLOCKS = 8
PIECES = 8
MESH = pl.DeviceIdType.MESH
EXACT = lax.Precision.HIGHEST
NT = (((1,), (1,)), ((), ()))
TN = (((0,), (0,)), ((), ()))


def most_steps(columns, limit):
    units = columns // LANES
    return max(s for s in range(1, limit + 1) if units % s == 0)


def select_matrix(shards, rows, folds, fold, owner_of):
    shape = (shards * rows, shards * folds * rows)
    row = lax.broadcasted_iota(jnp.int32, shape, 0)
    col = lax.broadcasted_iota(jnp.int32, shape, 1)
    total = jnp.zeros(shape, jnp.float32)
    for slot in range(shards):
        low = (slot * folds + fold) * rows
        hit = (col >= low) & (col < low + rows) & (row - col == owner_of(slot) * rows - low)
        total = total + jnp.where(hit, 1.0, 0.0)
    return total


def gather_kernel(
    shards, groups, folds, steps,
    p_ref, occ_ref, blk_ref, weights_ref, index_ref, table_ref,
    all_ref, hub_ref,
    raw, bands, held, acc, proj, proj_all, gram, gram_all,
    raw_sem, band_sem, out_sem, chip_send, core_send, recv, ga_send, ga_recv, sum_send, sum_recv,
):
    chips = shards // CORES
    rows, columns = p_ref.shape
    part = columns // folds
    width = part // steps
    packed = rows * folds
    n_occ, n_blk = occ_ref.shape[0], blk_ref.shape[0]
    me = lax.axis_index("band")
    chip, core = me // CORES, lax.rem(me, CORES)
    ga = lax.axis_index("ga")
    partner = chip * CORES + (1 - core)

    def band_at(distance):
        return lax.rem(chip + distance, chips) * CORES + core

    def owner_of(slot):
        return lax.rem(chip + slot // CORES, chips) * CORES + lax.rem(core + slot % CORES, CORES)

    def raw_copy(step, fold):
        return pltpu.make_async_copy(
            p_ref.at[:, pl.ds(pl.multiple_of(fold * part + step * width, LANES), width)],
            raw.at[lax.rem(step, 2), fold],
            raw_sem.at[lax.rem(step, 2), fold],
        )

    def band_copies(step):
        slot = lax.rem(step, 2)
        found = []
        for fold in range(folds):
            cols = pl.ds(pl.multiple_of(fold * part + step * width, LANES), width)
            found.append(pltpu.make_async_copy(
                occ_ref.at[:, cols], bands.at[slot, fold, pl.ds(0, n_occ)], band_sem.at[slot, fold, 0]))
            found.append(pltpu.make_async_copy(
                blk_ref.at[:, cols], bands.at[slot, fold, pl.ds(n_occ, n_blk)], band_sem.at[slot, fold, 1]))
        return found

    def rows_of(step, slot):
        return held.at[step, pl.ds(slot * packed, packed)]

    def to_chip(step, distance):
        slot = CORES * ((chips - distance) % chips)
        return pltpu.make_async_remote_copy(
            src_ref=rows_of(step, 0), dst_ref=rows_of(step, slot),
            send_sem=chip_send.at[step, distance], recv_sem=recv.at[step, slot],
            device_id={"band": band_at(distance)}, device_id_type=MESH)

    def to_core(step, distance):
        return pltpu.make_async_remote_copy(
            src_ref=rows_of(step, CORES * distance), dst_ref=rows_of(step, CORES * distance + 1),
            send_sem=core_send.at[step, distance], recv_sem=recv.at[step, CORES * distance + 1],
            device_id={"band": partner}, device_id_type=MESH)

    def keep(step):
        return pltpu.make_async_copy(
            held.at[step], all_ref.at[:, pl.ds(pl.multiple_of(step * width, LANES), width)], out_sem.at[step])

    for fold in range(folds):
        raw_copy(0, fold).start()
    for copy in band_copies(0):
        copy.start()
    acc[...] = jnp.zeros_like(acc)

    barrier = pltpu.get_barrier_semaphore()
    for k in range(1, shards):
        pl.semaphore_signal(barrier, inc=1, device_id={"band": lax.rem(me + k, shards)}, device_id_type=MESH)
    for k in range(1, groups):
        pl.semaphore_signal(barrier, inc=1, device_id={"ga": lax.rem(ga + k, groups)}, device_id_type=MESH)
    pl.semaphore_wait(barrier, shards + groups - 2)

    def send(step, carry):
        @pl.when(step + 1 < steps)
        def _():
            for fold in range(folds):
                raw_copy(step + 1, fold).start()

        for fold in range(folds):
            raw_copy(step, fold).wait()
        pieces = [raw[lax.rem(step, 2), fold].astype(jnp.float32) for fold in range(folds)]
        held[step, pl.ds(0, packed)] = jnp.concatenate(pieces, axis=0).astype(held.dtype)
        for distance in range(1, chips):
            to_chip(step, distance).start()
        to_core(step, 0).start()
        return carry

    lax.fori_loop(0, steps, send, 0)

    def use(step, carry):
        @pl.when(step + 1 < steps)
        def _():
            for copy in band_copies(step + 1):
                copy.start()

        for distance in range(1, chips):
            to_chip(step, chips - distance).wait_recv()
            to_core(step, distance).start()
        for copy in band_copies(step):
            copy.wait()
        for distance in range(chips):
            to_core(step, distance).wait_recv()
        keep(step).start()
        for fold in range(folds):
            acc[fold] += lax.dot_general(
                held[step], bands[lax.rem(step, 2), fold], NT, preferred_element_type=jnp.float32)
        return carry

    lax.fori_loop(0, steps, use, 0)

    selects = [select_matrix(shards, rows, folds, fold, owner_of) for fold in range(folds)]
    own = jnp.zeros(proj.shape, jnp.float32)
    for fold in range(folds):
        own = own + jnp.dot(selects[fold], acc[fold], precision=EXACT, preferred_element_type=jnp.float32)
    proj[...] = own

    def to_group(k):
        return pltpu.make_async_remote_copy(
            src_ref=proj, dst_ref=proj_all.at[k], send_sem=ga_send.at[k], recv_sem=ga_recv.at[k],
            device_id={"ga": lax.rem(ga + k, groups)}, device_id_type=MESH)

    for k in range(1, groups):
        to_group(k).start()
    for k in range(1, groups):
        to_group(k).wait_recv()
        own = own + proj_all[k]
    left = own[:, :n_occ] * weights_ref[...]
    occ = lax.dot_general(left, own[:, :n_occ], NT, precision=EXACT, preferred_element_type=jnp.float32)
    gram[...] = occ

    def to_band(k):
        return pltpu.make_async_remote_copy(
            src_ref=gram, dst_ref=gram_all.at[k], send_sem=sum_send.at[k], recv_sem=sum_recv.at[k],
            device_id={"band": lax.rem(me + k, shards)}, device_id_type=MESH)

    for k in range(1, shards):
        to_band(k).start()
    row = lax.broadcasted_iota(jnp.int32, occ.shape, 0)
    col = lax.broadcasted_iota(jnp.int32, occ.shape, 1)
    scale = jnp.zeros(occ.shape, jnp.float32)
    for atom in range(occ.shape[0] // ORB):
        low, high = atom * ORB, (atom + 1) * ORB
        inside = (row >= low) & (row < high) & (col >= low) & (col < high)
        scale = jnp.where(inside, table_ref[index_ref[atom]], scale)
    for k in range(1, shards):
        to_band(k).wait_recv()
        occ = occ + gram_all[k]
    potential = scale * (jnp.where(row == col, 0.5, 0.0) - occ)
    hub = jnp.dot(potential, own[:, n_occ:], precision=EXACT, preferred_element_type=jnp.float32)
    hub = hub.astype(jnp.bfloat16)
    for fold in range(folds):
        hub_ref[pl.ds(fold * n_blk, n_blk)] = lax.dot_general(
            hub, selects[fold].astype(jnp.bfloat16), TN, preferred_element_type=jnp.float32
        ).astype(jnp.bfloat16)

    def finish(step, carry):
        for distance in range(1, chips):
            to_chip(step, distance).wait_send()
        for distance in range(chips):
            to_core(step, distance).wait_send()
        keep(step).wait()
        return carry

    lax.fori_loop(0, steps, finish, 0)
    for k in range(1, groups):
        to_group(k).wait_send()
    for k in range(1, shards):
        to_band(k).wait_send()


def apply_kernel(folds, hub_ref, all_ref, out_ref, done, sems):
    step, steps = pl.program_id(0), pl.num_programs(0)
    width = all_ref.shape[1]
    bands = out_ref.shape[0]
    part = out_ref.shape[1] // folds
    slot = lax.rem(step, 2)

    def store(at, fold):
        return pltpu.make_async_copy(
            done.at[lax.rem(at, 2), pl.ds(fold * bands, bands)],
            out_ref.at[:, pl.ds(pl.multiple_of(fold * part + at * width, LANES), width)],
            sems.at[lax.rem(at, 2), fold],
        )

    @pl.when(step >= 2)
    def _():
        for fold in range(folds):
            store(step - 2, fold).wait()

    piece = width // most_steps(width, PIECES)
    for start in range(0, width, piece):
        cols = pl.ds(start, piece)
        done[slot, :, cols] = jnp.dot(
            hub_ref[...], all_ref[:, cols], preferred_element_type=jnp.float32
        ).astype(done.dtype)
    for fold in range(folds):
        store(step, fold).start()

    @pl.when(step == steps - 1)
    def _():
        @pl.when(step >= 1)
        def _():
            for fold in range(folds):
                store(step - 1, fold).wait()

        for fold in range(folds):
            store(step, fold).wait()


def per_device(shards, groups, projectors, occupied, block, weights, u_index, u_values):
    rows, columns = projectors.shape
    n_occ, n_blk = occupied.shape[0], block.shape[0]
    folds = SUBLANES // math.gcd(rows, SUBLANES)
    part = columns // folds
    steps = most_steps(part, STEPS)
    width = part // steps
    packed, total = rows * folds, rows * shards
    both = n_occ + n_blk
    anywhere = pl.BlockSpec(memory_space=pl.ANY)
    scalars = pl.BlockSpec(memory_space=pltpu.SMEM)
    vector = pl.BlockSpec(memory_space=pltpu.VMEM)
    dma = pltpu.SemaphoreType.DMA
    chips = shards // CORES
    gathered, hub = pl.pallas_call(
        functools.partial(gather_kernel, shards, groups, folds, steps),
        out_shape=(
            jax.ShapeDtypeStruct((shards * packed, part), projectors.dtype),
            jax.ShapeDtypeStruct((folds * n_blk, shards * packed), jnp.bfloat16),
        ),
        in_specs=[anywhere, anywhere, anywhere, vector, scalars, scalars],
        out_specs=(anywhere, vector),
        scratch_shapes=[
            pltpu.VMEM((2, folds, rows, width), projectors.dtype),
            pltpu.VMEM((2, folds, both, width), occupied.dtype),
            pltpu.VMEM((steps, shards * packed, width), projectors.dtype),
            pltpu.VMEM((folds, shards * packed, both), jnp.float32),
            pltpu.VMEM((total, both), jnp.float32),
            pltpu.VMEM((groups, total, both), jnp.float32),
            pltpu.VMEM((total, total), jnp.float32),
            pltpu.VMEM((shards, total, total), jnp.float32),
            dma((2, folds)),
            dma((2, folds, 2)),
            dma((steps,)),
            dma((steps, chips)),
            dma((steps, chips)),
            dma((steps, shards)),
            dma((groups,)),
            dma((groups,)),
            dma((shards,)),
            dma((shards,)),
        ],
        compiler_params=pltpu.CompilerParams(
            collective_id=0, has_side_effects=True, vmem_limit_bytes=56 * 2**20
        ),
        name="gather_project",
    )(projectors, occupied, block, weights.reshape(1, n_occ), u_index, u_values)

    blocks = most_steps(part, BLOCKS)
    tile = part // blocks
    return pl.pallas_call(
        functools.partial(apply_kernel, folds),
        grid=(blocks,),
        out_shape=jax.ShapeDtypeStruct((n_blk, columns), block.dtype),
        in_specs=[
            pl.BlockSpec((folds * n_blk, shards * packed), lambda i: (0, 0)),
            pl.BlockSpec((shards * packed, tile), lambda i: (0, i)),
        ],
        out_specs=anywhere,
        scratch_shapes=[
            pltpu.VMEM((2, folds * n_blk, tile), block.dtype),
            dma((2, folds)),
        ],
        name="apply_potential",
    )(hub, gathered)


def solution(mesh):
    spread = P(("image", "band"), "ga")
    in_specs = (spread, spread, spread, P(("image", "band")), P(), P())
    return jax.shard_map(
        functools.partial(per_device, mesh.shape["band"], mesh.shape["ga"]),
        mesh=mesh, in_specs=in_specs, out_specs=spread, check_vma=False,
    )
```

profile of v0, /device:TPU:0, one launch (start us, length us, event | category | flops | bytes accessed | tf_op | source)
XLA Modules:
  0.0 180.2 jit_solution(594982017435349351)
XLA Ops:
  0.0 160.9 %gather_project.1 = (bf16[160,81920]{1,0:T(8,128)(2,1)}, bf16[128,160]{1,0:T(8,128)(2,1)}) custom-call(bf16[20,163840]{1,0:T(8,128)(2,1)} %p_ref.1, bf16[32,163840]{1,0:T(8,128)(2,1)} %occ_ref.1, bf16[64,163840]{1,0:T(8,128)(2,1)} %blk_ref.1, f32[1,32]{1,0:T(1,128)} %bitcast.1, s32[16]{0:T(128)} %index_ref.1, f32[4]{0:T(128)} %table_ref.1), custom_call_target="tpu_custom_call" | custom-call | tf_op jit(solution)/shard_map/gather_project/pallas_call | solution.py:267
  160.9 19.3 %apply_potential.1 = bf16[64,163840]{1,0:T(8,128)(2,1)} custom-call(bf16[128,160]{1,0:T(8,128)(2,1)} %get-tuple-element.7.hub_ref, bf16[160,81920]{1,0:T(8,128)(2,1)} %get-tuple-element.8.all_ref), custom_call_target="tpu_custom_call" | custom-call | tf_op jit(solution)/shard_map/apply_potential/pallas_call | solution.py:303
where the time goes:
time: 181 us; the launch traced here: 180 us
  Pallas kernels  180 us (99%)
    pallas_call x1, Pallas kernels, per_device(): pl.pallas_call(functools.partial(gather_kernel, shards, groups, folds, st...  161 us
    pallas_call x1, Pallas kernels, per_device(): pl.pallas_call(functools.partial(apply_kernel, folds), grid=(blocks,), ou...  19.3 us

commit v1 on v0

v1 whole, which is shorter than its diff:
```python
import functools
import math

import jax
import jax.numpy as jnp
from jax import lax
from jax.experimental import pallas as pl
from jax.experimental.pallas import tpu as pltpu
from jax.sharding import PartitionSpec as P

ORB = 5
LANES = 128
SUBLANES = 8
CORES = 2
STEPS = 16
SMALL = 5
BLOCKS = 40
DEEP = 4
MESH = pl.DeviceIdType.MESH
NT = (((1,), (1,)), ((), ()))


def most_steps(columns, limit):
    units = columns // LANES
    return max(s for s in range(1, limit + 1) if units % s == 0)


def round_up(n, to):
    return -(-n // to) * to


def plan(part):
    steps = most_steps(part, STEPS)
    width = part // steps
    tail, left = [], width // LANES
    while left > SMALL:
        tail.append(left - left // 2)
        left //= 2
    tail.append(left)
    tail = [t * LANES for t in tail]
    starts = [(steps - 1) * width + sum(tail[:i]) for i in range(len(tail))]
    return steps - 1, width, list(zip(starts, tail))


def gather_kernel(
    shards, groups, folds,
    p_ref, occ_ref, blk_ref, weights_ref, index_ref, table_ref,
    all_ref, hub_ref,
    raw, bands, acc, proj, proj_all, diag, diag_all, select, scale, weight,
    raw_sem, band_sem, chip_send, core_send, recv, ga_send, ga_recv, sum_send, sum_recv,
):
    chips = shards // CORES
    rows, columns = p_ref.shape
    part = columns // folds
    packed = rows * folds
    main, width, tail = plan(part)
    count = main + len(tail)
    n_occ, n_blk = occ_ref.shape[0], blk_ref.shape[0]
    both = n_occ + n_blk
    total = shards * rows
    wide = bands.shape[2]
    lanes = proj.shape[1]
    me = lax.axis_index("band")
    chip, core = me // CORES, lax.rem(me, CORES)
    ga = lax.axis_index("ga")
    partner = chip * CORES + (1 - core)

    def band_at(distance):
        return lax.rem(chip + distance, chips) * CORES + core

    def span(step):
        if isinstance(step, int) and step >= main:
            return tail[step - main]
        return pl.multiple_of(step * width, LANES), width

    def raw_copy(step, fold):
        start, w = span(step)
        return pltpu.make_async_copy(
            p_ref.at[:, pl.ds(fold * part + start, w)],
            raw.at[fold, :, pl.ds(start, w)],
            raw_sem.at[step, fold],
        )

    def band_copies(step):
        start, w = span(step)
        slot = lax.rem(step, 2)
        found = []
        for fold in range(folds):
            cols = pl.ds(fold * part + start, w)
            found.append(pltpu.make_async_copy(
                occ_ref.at[:, cols], bands.at[slot, fold, pl.ds(0, n_occ), pl.ds(0, w)], band_sem.at[slot, fold, 0]))
            found.append(pltpu.make_async_copy(
                blk_ref.at[:, cols], bands.at[slot, fold, pl.ds(n_occ, n_blk), pl.ds(0, w)], band_sem.at[slot, fold, 1]))
        return found

    def rows_of(step, owner):
        start, w = span(step)
        return all_ref.at[pl.ds(pl.multiple_of(owner * packed, SUBLANES), packed), pl.ds(start, w)]

    def to_chip(step, distance):
        slot = CORES * ((chips - distance) % chips)
        return pltpu.make_async_remote_copy(
            src_ref=rows_of(step, me), dst_ref=rows_of(step, me),
            send_sem=chip_send.at[step, distance], recv_sem=recv.at[step, slot],
            device_id={"band": band_at(distance)}, device_id_type=MESH)

    def to_core(step, distance):
        return pltpu.make_async_remote_copy(
            src_ref=rows_of(step, band_at(distance)), dst_ref=rows_of(step, band_at(distance)),
            send_sem=core_send.at[step, distance], recv_sem=recv.at[step, CORES * distance + 1],
            device_id={"band": partner}, device_id_type=MESH)

    def pack(step):
        start, w = span(step)
        for fold in range(folds):
            raw_copy(step, fold).wait()
        pieces = [raw[fold, :, pl.ds(start, w)].astype(jnp.float32) for fold in range(folds)]
        all_ref[pl.ds(pl.multiple_of(me * packed, SUBLANES), packed), pl.ds(start, w)] = (
            jnp.concatenate(pieces, axis=0).astype(all_ref.dtype))

    def send(step):
        for distance in range(1, chips):
            to_chip(step, distance).start()
        to_core(step, 0).start()

    for fold in range(folds):
        raw_copy(0, fold).start()
    barrier = pltpu.get_barrier_semaphore()
    for k in range(1, shards):
        pl.semaphore_signal(barrier, inc=1, device_id={"band": lax.rem(me + k, shards)}, device_id_type=MESH)
    for k in range(1, groups):
        pl.semaphore_signal(barrier, inc=1, device_id={"ga": lax.rem(ga + k, groups)}, device_id_type=MESH)
    pack(0)
    pl.semaphore_wait(barrier, shards + groups - 2)
    send(0)

    def fetch(step):
        for fold in range(folds):
            raw_copy(step, fold).start()

    def loop(first, last, body):
        def run(step, carry):
            body(step)
            return carry
        lax.fori_loop(first, last, run, 0)

    loop(1, main, fetch)
    for step in range(max(main, 1), count):
        fetch(step)
    for copy in band_copies(0):
        copy.start()

    def pack_send(step):
        pack(step)
        send(step)

    loop(1, main, pack_send)
    for step in range(max(main, 1), count):
        pack_send(step)

    acc[...] = jnp.zeros_like(acc)
    if wide > both:
        for slot in range(2):
            for fold in range(folds):
                bands[slot, fold, pl.ds(both, wide - both)] = jnp.zeros((wide - both, width), bands.dtype)
    shape = (lanes, shards * packed)
    row = lax.broadcasted_iota(jnp.int32, shape, 0)
    col = lax.broadcasted_iota(jnp.int32, shape, 1)
    for fold in range(folds):
        hits = jnp.zeros(shape, jnp.float32)
        for owner in range(shards):
            low = owner * packed + fold * rows
            hit = (col >= low) & (col < low + rows) & (col - row == low - owner * rows)
            hits = hits + jnp.where(hit, 1.0, 0.0)
        select[fold] = hits.astype(select.dtype)
    lane = lax.broadcasted_iota(jnp.int32, (SUBLANES, lanes), 1)
    values = jnp.zeros((SUBLANES, lanes), jnp.float32)
    orbital = jnp.zeros((SUBLANES, lanes), jnp.int32)
    for atom in range(total // ORB):
        inside = (lane >= atom * ORB) & (lane < (atom + 1) * ORB)
        values = jnp.where(inside, table_ref[index_ref[atom]], values)
        orbital = jnp.where(inside, lane - atom * ORB, orbital)
    scale[...] = values
    one = lax.broadcasted_iota(jnp.int32, (n_occ, n_occ), 0)
    two = lax.broadcasted_iota(jnp.int32, (n_occ, n_occ), 1)
    column = jnp.sum(jnp.where(one == two, jnp.broadcast_to(weights_ref[...], (n_occ, n_occ)), 0.0), axis=1, keepdims=True)
    weight[...] = jnp.broadcast_to(column, weight.shape)

    def use(step):
        start, w = span(step)
        slot = lax.rem(step, 2)
        for distance in range(1, chips):
            to_chip(step, chips - distance).wait_recv()
            to_core(step, distance).start()
        for copy in band_copies(step):
            copy.wait()
        for distance in range(chips):
            to_core(step, distance).wait_recv()
        held = all_ref[:, pl.ds(start, w)]
        for fold in range(folds):
            acc[fold] += lax.dot_general(
                held, bands[slot, fold, :, pl.ds(0, w)], NT, preferred_element_type=jnp.float32)

    def sent(step):
        for distance in range(1, chips):
            to_chip(step, distance).wait_send()
        for distance in range(chips):
            to_core(step, distance).wait_send()

    def use_main(step):
        for copy in band_copies(step + 1):
            copy.start()
        use(step)
        sent(step)

    loop(0, main - 1, use_main)
    for step in range(max(main - 1, 0), count):
        if step + 1 < count:
            for copy in band_copies(step + 1):
                copy.start()
        use(step)

    pieces = []
    for owner in range(shards):
        piece = acc[0, pl.ds(owner * packed, rows)]
        for fold in range(1, folds):
            piece = piece + acc[fold, pl.ds(owner * packed + fold * rows, rows)]
        pieces.append(piece)
    if lanes > total:
        pieces.append(jnp.zeros((lanes - total, wide), jnp.float32))
    own = jnp.transpose(jnp.concatenate(pieces, axis=0))
    proj[...] = own

    def to_group(k, part_of):
        low, size = ((0, n_occ), (n_occ, n_blk))[part_of]
        return pltpu.make_async_remote_copy(
            src_ref=proj.at[pl.ds(low, size)], dst_ref=proj_all.at[k, pl.ds(low, size)],
            send_sem=ga_send.at[k, part_of], recv_sem=ga_recv.at[k, part_of],
            device_id={"ga": lax.rem(ga + k, groups)}, device_id_type=MESH)

    for part_of in range(2):
        for k in range(1, groups):
            to_group(k, part_of).start()
    for step in range(max(main - 1, 0), count):
        sent(step)
    mine = own[:n_occ]
    for k in range(1, groups):
        to_group(k, 0).wait_recv()
        mine = mine + proj_all[k, pl.ds(0, n_occ)]
    weighted = mine * weight[...]
    found = []
    for gap in range(ORB):
        moved = mine if gap == 0 else pltpu.roll(mine, lanes - gap, 1)
        found.append(jnp.sum(weighted * moved, axis=0, keepdims=True))
    found.append(jnp.zeros((SUBLANES - ORB, lanes), jnp.float32))
    occ = jnp.concatenate(found, axis=0)
    diag[...] = occ

    def to_band(k):
        return pltpu.make_async_remote_copy(
            src_ref=diag, dst_ref=diag_all.at[k], send_sem=sum_send.at[k], recv_sem=sum_recv.at[k],
            device_id={"band": lax.rem(me + k, shards)}, device_id_type=MESH)

    for k in range(1, shards):
        to_band(k).start()
    block = own[n_occ:both]
    for k in range(1, groups):
        to_group(k, 1).wait_recv()
        block = block + proj_all[k, pl.ds(n_occ, n_blk)]
    for k in range(1, shards):
        to_band(k).wait_recv()
        occ = occ + diag_all[k]
    u = scale[pl.ds(0, 1)]
    m = orbital[0:1]
    hub = (u * (0.5 - occ[0:1])) * block
    for gap in range(1, ORB):
        pair = -occ[gap:gap + 1]
        above = jnp.where(m + gap < ORB, u * pair, 0.0)
        below = jnp.where(m - gap >= 0, u * pltpu.roll(pair, gap, 1), 0.0)
        hub = hub + above * pltpu.roll(block, lanes - gap, 1) + below * pltpu.roll(block, gap, 1)
    hub = hub.astype(jnp.bfloat16)
    for fold in range(folds):
        hub_ref[pl.ds(fold * n_blk, n_blk)] = jnp.dot(
            hub, select[fold], preferred_element_type=jnp.float32).astype(jnp.bfloat16)

    for k in range(1, groups):
        for part_of in range(2):
            to_group(k, part_of).wait_send()
    for k in range(1, shards):
        to_band(k).wait_send()


def apply_kernel(folds, blocks, hub_ref, all_ref, out_ref, done, sems):
    bands = out_ref.shape[0]
    part = out_ref.shape[1] // folds
    tile = part // blocks
    deep = done.shape[0]

    def stores(step):
        slot = lax.rem(step, deep)
        start = pl.multiple_of(step * tile, LANES)
        return [pltpu.make_async_copy(
            done.at[slot, pl.ds(fold * bands, bands)],
            out_ref.at[:, pl.ds(fold * part + start, tile)],
            sems.at[slot, fold],
        ) for fold in range(folds)]

    def run(step, carry):
        @pl.when(step >= deep)
        def _():
            for copy in stores(step - deep):
                copy.wait()

        done[lax.rem(step, deep)] = jnp.dot(
            hub_ref[...], all_ref[:, pl.ds(pl.multiple_of(step * tile, LANES), tile)],
            preferred_element_type=jnp.float32).astype(done.dtype)
        for copy in stores(step):
            copy.start()
        return carry

    lax.fori_loop(0, blocks, run, 0)
    for step in range(max(blocks - deep, 0), blocks):
        for copy in stores(step):
            copy.wait()


def per_device(shards, groups, projectors, occupied, block, weights, u_index, u_values):
    rows, columns = projectors.shape
    n_occ, n_blk = occupied.shape[0], block.shape[0]
    folds = SUBLANES // math.gcd(rows, SUBLANES)
    part = columns // folds
    main, width, tail = plan(part)
    count = main + len(tail)
    packed, total = rows * folds, rows * shards
    wide = round_up(n_occ + n_blk, LANES)
    lanes = round_up(total, LANES)
    anywhere = pl.BlockSpec(memory_space=pl.ANY)
    scalars = pl.BlockSpec(memory_space=pltpu.SMEM)
    vector = pl.BlockSpec(memory_space=pltpu.VMEM)
    dma = pltpu.SemaphoreType.DMA
    chips = shards // CORES
    gathered, hub = pl.pallas_call(
        functools.partial(gather_kernel, shards, groups, folds),
        out_shape=(
            pltpu.VMEM((shards * packed, part), projectors.dtype),
            pltpu.VMEM((folds * n_blk, shards * packed), jnp.bfloat16),
        ),
        in_specs=[anywhere, anywhere, anywhere, vector, scalars, scalars],
        out_specs=(vector, vector),
        scratch_shapes=[
            pltpu.VMEM((folds, rows, part), projectors.dtype),
            pltpu.VMEM((2, folds, wide, width), occupied.dtype),
            pltpu.VMEM((folds, shards * packed, wide), jnp.float32),
            pltpu.VMEM((wide, lanes), jnp.float32),
            pltpu.VMEM((groups, wide, lanes), jnp.float32),
            pltpu.VMEM((SUBLANES, lanes), jnp.float32),
            pltpu.VMEM((shards, SUBLANES, lanes), jnp.float32),
            pltpu.VMEM((folds, lanes, shards * packed), jnp.bfloat16),
            pltpu.VMEM((SUBLANES, lanes), jnp.float32),
            pltpu.VMEM((n_occ, lanes), jnp.float32),
            dma((count, folds)),
            dma((2, folds, 2)),
            dma((count, chips)),
            dma((count, chips)),
            dma((count, shards)),
            dma((groups, 2)),
            dma((groups, 2)),
            dma((shards,)),
            dma((shards,)),
        ],
        compiler_params=pltpu.CompilerParams(
            collective_id=0, has_side_effects=True, vmem_limit_bytes=24 * 2**20
        ),
        name="gather_project",
    )(projectors, occupied, block, weights.reshape(1, n_occ), u_index, u_values)

    blocks = most_steps(part, BLOCKS)
    tile = part // blocks
    deep = min(DEEP, blocks)
    return pl.pallas_call(
        functools.partial(apply_kernel, folds, blocks),
        out_shape=jax.ShapeDtypeStruct((n_blk, columns), block.dtype),
        in_specs=[vector, vector],
        out_specs=anywhere,
        scratch_shapes=[
            pltpu.VMEM((deep, folds * n_blk, tile), block.dtype),
            dma((deep, folds)),
        ],
        compiler_params=pltpu.CompilerParams(vmem_limit_bytes=24 * 2**20),
        name="apply_potential",
    )(hub, gathered)


def solution(mesh):
    spread = P(("image", "band"), "ga")
    in_specs = (spread, spread, spread, P(("image", "band")), P(), P())
    return jax.shard_map(
        functools.partial(per_device, mesh.shape["band"], mesh.shape["ga"]),
        mesh=mesh, in_specs=in_specs, out_specs=spread, check_vma=False,
    )
```

time: 181 us -> 191 us (1.055)
  local copies, waits for them, and re-layouts: 0 us -> 19.1 us
  Pallas kernels: 180 us -> 171 us
    unnamed x0 -> x10, local copies, waits for them, and re-layouts: none -> 19.1 us
    pallas_call x2, Pallas kernels: 180 us -> 171 us  [the longest x1 159 us: per_device(): pl.pallas_call(functools.partial(gather_kernel, shards, groups, folds), o...]
where the time goes in v1:
time: 191 us; the launch traced here: 190 us
  Pallas kernels  171 us (90%)
  local copies, waits for them, and re-layouts  19.1 us (10%)
    pallas_call x1, Pallas kernels, per_device(): pl.pallas_call(functools.partial(gather_kernel, shards, groups, folds), o...  159 us
    unnamed x10, local copies, waits for them, and re-layouts  19.1 us
    pallas_call x1, Pallas kernels, per_device(): pl.pallas_call(functools.partial(apply_kernel, folds, blocks), out_shape=...  12.8 us

profile of v1, /device:TPU:0, one launch (start us, length us, event | category | flops | bytes accessed | tf_op | source)
XLA Modules:
  0.0 190.5 jit_solution(13163835413020496302)
XLA Ops:
  0.0 0.0 copy-start.2
  0.0 0.7 copy-done.2
  0.7 0.0 copy-start.3
  0.7 0.7 copy-done.3
  1.3 0.0 copy-start.4
  1.3 0.7 copy-done.4
  2.0 158.6 %gather_project.1 = (bf16[160,81920]{1,0:T(8,128)(2,1)S(1)}, bf16[128,160]{1,0:T(8,128)(2,1)S(1)}) custom-call(bf16[20,163840]{1,0:T(8,128)(2,1)} %p_ref.1, bf16[32,163840]{1,0:T(8,128)(2,1)} %occ_ref.1, bf16[64,163840]{1,0:T(8,128)(2,1)} %blk_ref.1, f32[1,32]{1,0:T(1,128)S(1)} %bitcast.1, s32[16]{0:T(128)S(1)} %copy-done.3, f32[4]{0:T(128)S(1)} %copy-done.4), custom_call_target="tpu_custom_call" | custom-call | tf_op jit(solution)/shard_map/gather_project/pallas_call | solution.py:342
  160.6 0.0 copy-start
  160.6 8.6 %copy-done = bf16[160,81920]{1,0:T(8,128)(2,1)} copy-done((bf16[160,81920]{1,0:T(8,128)(2,1)}, bf16[160,81920]{1,0:T(8,128)(2,1)S(1)}, u32[]{:S(2)}) %copy-start) | copy-done | bytes 26214424
  169.2 0.0 copy-start.1
  169.2 8.5 %copy-done.1 = bf16[160,81920]{1,0:T(8,128)(2,1)S(1)} copy-done((bf16[160,81920]{1,0:T(8,128)(2,1)S(1)}, bf16[160,81920]{1,0:T(8,128)(2,1)}, u32[]{:S(2)}) %copy-start.1) | copy-done | bytes 26214424
  177.7 12.8 %apply_potential.1 = bf16[64,163840]{1,0:T(8,128)(2,1)} custom-call(bf16[128,160]{1,0:T(8,128)(2,1)S(1)} %get-tuple-element.7.hub_ref, bf16[160,81920]{1,0:T(8,128)(2,1)S(1)} %copy-done.1), custom_call_target="tpu_custom_call" | custom-call | tf_op jit(solution)/shard_map/apply_potential/pallas_call | solution.py:380
Async XLA Ops:
  0.0 0.7 copy-start.2
  0.7 0.7 copy-start.3
  1.3 0.7 copy-start.4
  160.6 8.6 %copy-start = (bf16[160,81920]{1,0:T(8,128)(2,1)}, bf16[160,81920]{1,0:T(8,128)(2,1)S(1)}, u32[]{:S(2)}) copy-start(bf16[160,81920]{1,0:T(8,128)(2,1)S(1)} %get-tuple-element.8.all_ref) | copy-start | bytes 78643200
  169.2 8.5 %copy-start.1 = (bf16[160,81920]{1,0:T(8,128)(2,1)S(1)}, bf16[160,81920]{1,0:T(8,128)(2,1)}, u32[]{:S(2)}) copy-start(bf16[160,81920]{1,0:T(8,128)(2,1)} %copy-done) | copy-start | bytes 78643200

commit v2 on v1

--- a/solution.py
+++ b/solution.py
@@ -44,10 +44,10 @@
 
 def gather_kernel(
     shards, groups, folds,
-    p_ref, occ_ref, blk_ref, weights_ref, index_ref, table_ref,
+    p_ref, occ_ref, blk_ref, weights_hbm, index_hbm, table_hbm,
     all_ref, hub_ref,
-    raw, bands, acc, proj, proj_all, diag, diag_all, select, scale, weight,
-    raw_sem, band_sem, chip_send, core_send, recv, ga_send, ga_recv, sum_send, sum_recv,
+    weights_ref, index_ref, table_ref, raw, bands, acc, proj, proj_all, diag, diag_all, select, scale, weight,
+    small_sem, raw_sem, band_sem, chip_send, core_send, recv, ga_send, ga_recv, sum_send, sum_recv,
 ):
     chips = shards // CORES
     rows, columns = p_ref.shape
@@ -134,6 +134,14 @@
     pl.semaphore_wait(barrier, shards + groups - 2)
     send(0)
 
+    small = [
+        pltpu.make_async_copy(source, target, small_sem.at[k])
+        for k, (source, target) in enumerate(
+            ((weights_hbm, weights_ref), (index_hbm, index_ref), (table_hbm, table_ref)))
+    ]
+    for copy in small:
+        copy.start()
+
     def fetch(step):
         for fold in range(folds):
             raw_copy(step, fold).start()
@@ -173,6 +181,8 @@
             hit = (col >= low) & (col < low + rows) & (col - row == low - owner * rows)
             hits = hits + jnp.where(hit, 1.0, 0.0)
         select[fold] = hits.astype(select.dtype)
+    for copy in small:
+        copy.wait()
     lane = lax.broadcasted_iota(jnp.int32, (SUBLANES, lanes), 1)
     values = jnp.zeros((SUBLANES, lanes), jnp.float32)
     orbital = jnp.zeros((SUBLANES, lanes), jnp.int32)
@@ -335,7 +345,6 @@
     wide = round_up(n_occ + n_blk, LANES)
     lanes = round_up(total, LANES)
     anywhere = pl.BlockSpec(memory_space=pl.ANY)
-    scalars = pl.BlockSpec(memory_space=pltpu.SMEM)
     vector = pl.BlockSpec(memory_space=pltpu.VMEM)
     dma = pltpu.SemaphoreType.DMA
     chips = shards // CORES
@@ -345,9 +354,12 @@
             pltpu.VMEM((shards * packed, part), projectors.dtype),
             pltpu.VMEM((folds * n_blk, shards * packed), jnp.bfloat16),
         ),
-        in_specs=[anywhere, anywhere, anywhere, vector, scalars, scalars],
+        in_specs=[anywhere] * 6,
         out_specs=(vector, vector),
         scratch_shapes=[
+            pltpu.VMEM((1, n_occ), jnp.float32),
+            pltpu.SMEM(u_index.shape, u_index.dtype),
+            pltpu.SMEM(u_values.shape, u_values.dtype),
             pltpu.VMEM((folds, rows, part), projectors.dtype),
             pltpu.VMEM((2, folds, wide, width), occupied.dtype),
             pltpu.VMEM((folds, shards * packed, wide), jnp.float32),
@@ -358,6 +370,7 @@
             pltpu.VMEM((folds, lanes, shards * packed), jnp.bfloat16),
             pltpu.VMEM((SUBLANES, lanes), jnp.float32),
             pltpu.VMEM((n_occ, lanes), jnp.float32),
+            dma((3,)),
             dma((count, folds)),
             dma((2, folds, 2)),
             dma((count, chips)),
@@ -372,7 +385,11 @@
             collective_id=0, has_side_effects=True, vmem_limit_bytes=24 * 2**20
         ),
         name="gather_project",
-    )(projectors, occupied, block, weights.reshape(1, n_occ), u_index, u_values)
+    )(*[
+        pltpu.with_memory_space_constraint(a, pltpu.HBM)
+        for a in (projectors, occupied, block, weights.reshape(1, n_occ), u_index, u_values)
+    ])
+    gathered, hub = [pltpu.with_memory_space_constraint(a, pltpu.VMEM) for a in (gathered, hub)]
 
     blocks = most_steps(part, BLOCKS)
     tile = part // blocks

time: 191 us -> 171 us (0.90)
  local copies, waits for them, and re-layouts: 19.1 us -> 0 us
    unnamed x10 -> x0, local copies, waits for them, and re-layouts: 19.1 us -> none
where the time goes in v2:
time: 171 us
  Pallas kernels  171 us (100%)
    pallas_call x1, Pallas kernels, per_device(): pl.pallas_call(functools.partial(gather_kernel, shards, groups, folds), o...  158 us
    pallas_call x1, Pallas kernels, per_device(): pl.pallas_call(functools.partial(apply_kernel, folds, blocks), out_shape=...  12.7 us

profile of v2, /device:TPU:0, one launch (start us, length us, event | category | flops | bytes accessed | tf_op | source)
XLA Modules:
  0.0 170.7 jit_solution(17854839239022287104)
XLA Ops:
  0.0 158.0 %gather_project.1 = (bf16[160,81920]{1,0:T(8,128)(2,1)S(1)}, bf16[128,160]{1,0:T(8,128)(2,1)S(1)}) custom-call(bf16[20,163840]{1,0:T(8,128)(2,1)} %p_ref.1, bf16[32,163840]{1,0:T(8,128)(2,1)} %occ_ref.1, bf16[64,163840]{1,0:T(8,128)(2,1)} %blk_ref.1, f32[1,32]{1,0:T(1,128)} %bitcast.1, s32[16]{0:T(128)} %index_hbm.1, f32[4]{0:T(128)} %table_hbm.1), custom_call_target="tpu_custom_call" | custom-call | tf_op jit(solution)/shard_map/gather_project/pallas_call | solution.py:351
  158.0 12.7 %apply_potential.1 = bf16[64,163840]{1,0:T(8,128)(2,1)} custom-call(bf16[128,160]{1,0:T(8,128)(2,1)S(1)} %get-tuple-element.7.hub_ref, bf16[160,81920]{1,0:T(8,128)(2,1)S(1)} %get-tuple-element.8.all_ref), custom_call_target="tpu_custom_call" | custom-call | tf_op jit(solution)/shard_map/apply_potential/pallas_call | solution.py:397

commit v3 on v2

--- a/solution.py
+++ b/solution.py
@@ -12,10 +12,11 @@
 LANES = 128
 SUBLANES = 8
 CORES = 2
-STEPS = 16
-SMALL = 5
-BLOCKS = 40
-DEEP = 4
+STEPS = 10
+SMALL = 8
+BLOCKS = 5
+PIECES = 16
+DEEP = 2
 MESH = pl.DeviceIdType.MESH
 NT = (((1,), (1,)), ((), ()))
 
@@ -32,14 +33,23 @@
 def plan(part):
     steps = most_steps(part, STEPS)
     width = part // steps
-    tail, left = [], width // LANES
+    units = width // LANES
+    first = units // 8
+    head = [first, units - first] if first and steps > 1 else [units]
+    last, left = [], units
     while left > SMALL:
-        tail.append(left - left // 2)
+        last.append(left - left // 2)
         left //= 2
-    tail.append(left)
-    tail = [t * LANES for t in tail]
-    starts = [(steps - 1) * width + sum(tail[:i]) for i in range(len(tail))]
-    return steps - 1, width, list(zip(starts, tail))
+    last.append(left)
+    sends = []
+    for step, cuts in ((0, head),) * (steps > 1) + ((steps - 1, last),):
+        at = step * width
+        for cut in cuts:
+            sends.append((step, at, cut * LANES))
+            at += cut * LANES
+    heads = [x for x in sends if x[0] == 0 and steps > 1]
+    tails = [x for x in sends if x[0] == steps - 1]
+    return steps, width, heads, tails
 
 
 def gather_kernel(
@@ -53,8 +63,10 @@
     rows, columns = p_ref.shape
     part = columns // folds
     packed = rows * folds
-    main, width, tail = plan(part)
-    count = main + len(tail)
+    steps, width, heads, tails = plan(part)
+    middle = max(steps - 2, 0)
+    count = len(heads) + middle + len(tails)
+    first_tail = len(heads) + middle
     n_occ, n_blk = occ_ref.shape[0], blk_ref.shape[0]
     both = n_occ + n_blk
     total = shards * rows
@@ -68,29 +80,30 @@
     def band_at(distance):
         return lax.rem(chip + distance, chips) * CORES + core
 
-    def span(step):
-        if isinstance(step, int) and step >= main:
-            return tail[step - main]
-        return pl.multiple_of(step * width, LANES), width
-
-    def raw_copy(step, fold):
-        start, w = span(step)
+    def span(piece):
+        if isinstance(piece, int) and piece < len(heads):
+            return heads[piece][1:]
+        if isinstance(piece, int) and piece >= first_tail:
+            return tails[piece - first_tail][1:]
+        return pl.multiple_of((piece - len(heads) + 1) * width, LANES), width
+
+    def raw_copy(piece, fold):
+        start, w = span(piece)
         return pltpu.make_async_copy(
             p_ref.at[:, pl.ds(fold * part + start, w)],
             raw.at[fold, :, pl.ds(start, w)],
-            raw_sem.at[step, fold],
+            raw_sem.at[piece, fold],
         )
 
     def band_copies(step):
-        start, w = span(step)
         slot = lax.rem(step, 2)
         found = []
         for fold in range(folds):
-            cols = pl.ds(fold * part + start, w)
+            cols = pl.ds(pl.multiple_of(fold * part + step * width, LANES), width)
             found.append(pltpu.make_async_copy(
-                occ_ref.at[:, cols], bands.at[slot, fold, pl.ds(0, n_occ), pl.ds(0, w)], band_sem.at[slot, fold, 0]))
+                occ_ref.at[:, cols], bands.at[slot, fold, pl.ds(0, n_occ)], band_sem.at[slot, fold, 0]))
             found.append(pltpu.make_async_copy(
-                blk_ref.at[:, cols], bands.at[slot, fold, pl.ds(n_occ, n_blk), pl.ds(0, w)], band_sem.at[slot, fold, 1]))
+                blk_ref.at[:, cols], bands.at[slot, fold, pl.ds(n_occ, n_blk)], band_sem.at[slot, fold, 1]))
         return found
 
     def rows_of(step, owner):
@@ -152,20 +165,23 @@
             return carry
         lax.fori_loop(first, last, run, 0)
 
-    loop(1, main, fetch)
-    for step in range(max(main, 1), count):
-        fetch(step)
-    for copy in band_copies(0):
-        copy.start()
-
-    def pack_send(step):
-        pack(step)
-        send(step)
-
-    loop(1, main, pack_send)
-    for step in range(max(main, 1), count):
-        pack_send(step)
-
+    def each(body, low):
+        for piece in range(low, len(heads)):
+            body(piece)
+        loop(max(low, len(heads)), first_tail, body)
+        for piece in range(max(low, first_tail), count):
+            body(piece)
+
+    each(fetch, 1)
+    for step in range(min(2, steps)):
+        for copy in band_copies(step):
+            copy.start()
+
+    def pack_send(piece):
+        pack(piece)
+        send(piece)
+
+    each(pack_send, 1)
     acc[...] = jnp.zeros_like(acc)
     if wide > both:
         for slot in range(2):
@@ -196,39 +212,71 @@
     column = jnp.sum(jnp.where(one == two, jnp.broadcast_to(weights_ref[...], (n_occ, n_occ)), 0.0), axis=1, keepdims=True)
     weight[...] = jnp.broadcast_to(column, weight.shape)
 
-    def use(step):
-        start, w = span(step)
+    def forward(piece):
+        for distance in range(1, chips):
+            to_chip(piece, chips - distance).wait_recv()
+            to_core(piece, distance).start()
+
+    def project(piece, step, low):
+        start, w = span(piece)
         slot = lax.rem(step, 2)
-        for distance in range(1, chips):
-            to_chip(step, chips - distance).wait_recv()
-            to_core(step, distance).start()
-        for copy in band_copies(step):
-            copy.wait()
         for distance in range(chips):
-            to_core(step, distance).wait_recv()
+            to_core(piece, distance).wait_recv()
         held = all_ref[:, pl.ds(start, w)]
         for fold in range(folds):
             acc[fold] += lax.dot_general(
-                held, bands[slot, fold, :, pl.ds(0, w)], NT, preferred_element_type=jnp.float32)
-
-    def sent(step):
+                held, bands[slot, fold, :, pl.ds(low, w)], NT, preferred_element_type=jnp.float32)
+
+    def sent(piece):
         for distance in range(1, chips):
-            to_chip(step, distance).wait_send()
+            to_chip(piece, distance).wait_send()
         for distance in range(chips):
-            to_core(step, distance).wait_send()
-
-    def use_main(step):
-        for copy in band_copies(step + 1):
+            to_core(piece, distance).wait_send()
+
+    def landed(step):
+        for copy in band_copies(step):
+            copy.wait()
+
+    def ahead(step):
+        for copy in band_copies(step):
             copy.start()
-        use(step)
-        sent(step)
-
-    loop(0, main - 1, use_main)
-    for step in range(max(main - 1, 0), count):
-        if step + 1 < count:
-            for copy in band_copies(step + 1):
-                copy.start()
-        use(step)
+
+    waiting = None
+    for piece, (step, start, _) in enumerate(heads):
+        forward(piece)
+        if waiting is not None:
+            project(*waiting)
+        elif piece == 0:
+            landed(0)
+        waiting = (piece, 0, start)
+    if middle:
+        piece = len(heads)
+        forward(piece)
+        project(*waiting)
+        for each_one in range(len(heads)):
+            sent(each_one)
+        ahead(2)
+
+        def step_on(step):
+            piece = step - 1 + len(heads)
+            forward(piece)
+            landed(step - 1)
+            project(piece - 1, step - 1, 0)
+            sent(piece - 1)
+            ahead(step + 1)
+
+        loop(2, steps - 1, step_on)
+        waiting = (first_tail - 1, steps - 2, 0)
+    for piece in range(first_tail, count):
+        forward(piece)
+        if piece == first_tail and middle:
+            landed(steps - 2)
+        if waiting is not None:
+            project(*waiting)
+        if piece == first_tail:
+            landed(steps - 1)
+        waiting = (piece, steps - 1, tails[piece - first_tail][1] - (steps - 1) * width)
+    project(*waiting)
 
     pieces = []
     for owner in range(shards):
@@ -251,8 +299,8 @@
     for part_of in range(2):
         for k in range(1, groups):
             to_group(k, part_of).start()
-    for step in range(max(main - 1, 0), count):
-        sent(step)
+    for piece in range(max(first_tail - 1, 0) if middle else 0, count):
+        sent(piece)
     mine = own[:n_occ]
     for k in range(1, groups):
         to_group(k, 0).wait_recv()
@@ -300,38 +348,43 @@
         to_band(k).wait_send()
 
 
-def apply_kernel(folds, blocks, hub_ref, all_ref, out_ref, done, sems):
+def apply_kernel(folds, blocks, pieces, hub_ref, all_ref, out_ref, done, sems):
     bands = out_ref.shape[0]
     part = out_ref.shape[1] // folds
     tile = part // blocks
+    size = tile // pieces
     deep = done.shape[0]
 
-    def stores(step):
+    def stores(step, piece):
         slot = lax.rem(step, deep)
-        start = pl.multiple_of(step * tile, LANES)
+        start = pl.multiple_of(step * tile, LANES) + piece * size
         return [pltpu.make_async_copy(
-            done.at[slot, pl.ds(fold * bands, bands)],
-            out_ref.at[:, pl.ds(fold * part + start, tile)],
-            sems.at[slot, fold],
+            done.at[slot, pl.ds(fold * bands, bands), pl.ds(piece * size, size)],
+            out_ref.at[:, pl.ds(pl.multiple_of(fold * part + start, LANES), size)],
+            sems.at[slot, piece, fold],
         ) for fold in range(folds)]
 
     def run(step, carry):
         @pl.when(step >= deep)
         def _():
-            for copy in stores(step - deep):
-                copy.wait()
-
-        done[lax.rem(step, deep)] = jnp.dot(
-            hub_ref[...], all_ref[:, pl.ds(pl.multiple_of(step * tile, LANES), tile)],
-            preferred_element_type=jnp.float32).astype(done.dtype)
-        for copy in stores(step):
-            copy.start()
+            for piece in range(pieces):
+                for copy in stores(step - deep, piece):
+                    copy.wait()
+
+        for piece in range(pieces):
+            start = pl.multiple_of(step * tile + piece * size, LANES)
+            done[lax.rem(step, deep), :, pl.ds(piece * size, size)] = jnp.dot(
+                hub_ref[...], all_ref[:, pl.ds(start, size)],
+                preferred_element_type=jnp.float32).astype(done.dtype)
+            for copy in stores(step, piece):
+                copy.start()
         return carry
 
     lax.fori_loop(0, blocks, run, 0)
     for step in range(max(blocks - deep, 0), blocks):
-        for copy in stores(step):
-            copy.wait()
+        for piece in range(pieces):
+            for copy in stores(step, piece):
+                copy.wait()
 
 
 def per_device(shards, groups, projectors, occupied, block, weights, u_index, u_values):
@@ -339,8 +392,8 @@
     n_occ, n_blk = occupied.shape[0], block.shape[0]
     folds = SUBLANES // math.gcd(rows, SUBLANES)
     part = columns // folds
-    main, width, tail = plan(part)
-    count = main + len(tail)
+    steps, width, heads, tails = plan(part)
+    count = len(heads) + max(steps - 2, 0) + len(tails)
     packed, total = rows * folds, rows * shards
     wide = round_up(n_occ + n_blk, LANES)
     lanes = round_up(total, LANES)
@@ -393,15 +446,16 @@
 
     blocks = most_steps(part, BLOCKS)
     tile = part // blocks
+    pieces = most_steps(tile, PIECES)
     deep = min(DEEP, blocks)
     return pl.pallas_call(
-        functools.partial(apply_kernel, folds, blocks),
+        functools.partial(apply_kernel, folds, blocks, pieces),
         out_shape=jax.ShapeDtypeStruct((n_blk, columns), block.dtype),
         in_specs=[vector, vector],
         out_specs=anywhere,
         scratch_shapes=[
             pltpu.VMEM((deep, folds * n_blk, tile), block.dtype),
-            dma((deep, folds)),
+            dma((deep, pieces, folds)),
         ],
         compiler_params=pltpu.CompilerParams(vmem_limit_bytes=24 * 2**20),
         name="apply_potential",

time: 171 us -> 164 us (0.959)
  Pallas kernels: 171 us -> 164 us
    pallas_call x1, Pallas kernels: 12.7 us -> 7.87 us  [per_device(): pl.pallas_call(functools.partial(apply_kernel, folds, blocks, pieces), ou...]
    pallas_call x1, Pallas kernels: 158 us -> 156 us  [per_device(): pl.pallas_call(functools.partial(gather_kernel, shards, groups, folds), o...]
where the time goes in v3:
time: 164 us
  Pallas kernels  164 us (100%)
    pallas_call x1, Pallas kernels, per_device(): pl.pallas_call(functools.partial(gather_kernel, shards, groups, folds), o...  156 us
    pallas_call x1, Pallas kernels, per_device(): pl.pallas_call(functools.partial(apply_kernel, folds, blocks, pieces), ou...  7.87 us

profile of v3, /device:TPU:0, one launch (start us, length us, event | category | flops | bytes accessed | tf_op | source)
XLA Modules:
  0.0 164.0 jit_solution(16684336755892087335)
XLA Ops:
  0.0 156.1 %gather_project.1 = (bf16[160,81920]{1,0:T(8,128)(2,1)S(1)}, bf16[128,160]{1,0:T(8,128)(2,1)S(1)}) custom-call(bf16[20,163840]{1,0:T(8,128)(2,1)} %p_ref.1, bf16[32,163840]{1,0:T(8,128)(2,1)} %occ_ref.1, bf16[64,163840]{1,0:T(8,128)(2,1)} %blk_ref.1, f32[1,32]{1,0:T(1,128)} %bitcast.1, s32[16]{0:T(128)} %index_hbm.1, f32[4]{0:T(128)} %table_hbm.1), custom_call_target="tpu_custom_call" | custom-call | tf_op jit(solution)/shard_map/gather_project/pallas_call | solution.py:404
  156.1 7.9 %apply_potential.1 = bf16[64,163840]{1,0:T(8,128)(2,1)} custom-call(bf16[128,160]{1,0:T(8,128)(2,1)S(1)} %get-tuple-element.7.hub_ref, bf16[160,81920]{1,0:T(8,128)(2,1)S(1)} %get-tuple-element.8.all_ref), custom_call_target="tpu_custom_call" | custom-call | tf_op jit(solution)/shard_map/apply_potential/pallas_call | solution.py:451

commit v4 on v3

--- a/solution.py
+++ b/solution.py
@@ -15,7 +15,7 @@
 STEPS = 10
 SMALL = 8
 BLOCKS = 5
-PIECES = 16
+PIECES = 8
 DEEP = 2
 MESH = pl.DeviceIdType.MESH
 NT = (((1,), (1,)), ((), ()))
@@ -325,17 +325,20 @@
     for k in range(1, groups):
         to_group(k, 1).wait_recv()
         block = block + proj_all[k, pl.ds(n_occ, n_blk)]
+    u = scale[pl.ds(0, 1)]
+    m = orbital[0:1]
+    terms = []
+    for gap in range(1, ORB):
+        terms.append((
+            jnp.where(m + gap < ORB, u, 0.0), pltpu.roll(block, lanes - gap, 1),
+            jnp.where(m - gap >= 0, u, 0.0), pltpu.roll(block, gap, 1)))
     for k in range(1, shards):
         to_band(k).wait_recv()
         occ = occ + diag_all[k]
-    u = scale[pl.ds(0, 1)]
-    m = orbital[0:1]
     hub = (u * (0.5 - occ[0:1])) * block
-    for gap in range(1, ORB):
-        pair = -occ[gap:gap + 1]
-        above = jnp.where(m + gap < ORB, u * pair, 0.0)
-        below = jnp.where(m - gap >= 0, u * pltpu.roll(pair, gap, 1), 0.0)
-        hub = hub + above * pltpu.roll(block, lanes - gap, 1) + below * pltpu.roll(block, gap, 1)
+    for gap, (u_above, above, u_below, below) in enumerate(terms, 1):
+        pair = occ[gap:gap + 1]
+        hub = hub - (u_above * pair) * above - (u_below * pltpu.roll(pair, gap, 1)) * below
     hub = hub.astype(jnp.bfloat16)
     for fold in range(folds):
         hub_ref[pl.ds(fold * n_blk, n_blk)] = jnp.dot(

time: 164 us -> 164 us (level)
  no operation moved by 1% of the time
where the time goes in v4:
time: 164 us
  Pallas kernels  164 us (100%)
    pallas_call x1, Pallas kernels, per_device(): pl.pallas_call(functools.partial(gather_kernel, shards, groups, folds), o...  156 us
    pallas_call x1, Pallas kernels, per_device(): pl.pallas_call(functools.partial(apply_kernel, folds, blocks, pieces), ou...  7.61 us

profile of v4, /device:TPU:0, one launch (start us, length us, event | category | flops | bytes accessed | tf_op | source)
XLA Modules:
  0.0 163.7 jit_solution(12726299930207638610)
XLA Ops:
  0.0 156.1 %gather_project.1 = (bf16[160,81920]{1,0:T(8,128)(2,1)S(1)}, bf16[128,160]{1,0:T(8,128)(2,1)S(1)}) custom-call(bf16[20,163840]{1,0:T(8,128)(2,1)} %p_ref.1, bf16[32,163840]{1,0:T(8,128)(2,1)} %occ_ref.1, bf16[64,163840]{1,0:T(8,128)(2,1)} %blk_ref.1, f32[1,32]{1,0:T(1,128)} %bitcast.1, s32[16]{0:T(128)} %index_hbm.1, f32[4]{0:T(128)} %table_hbm.1), custom_call_target="tpu_custom_call" | custom-call | tf_op jit(solution)/shard_map/gather_project/pallas_call | solution.py:407
  156.1 7.6 %apply_potential.1 = bf16[64,163840]{1,0:T(8,128)(2,1)} custom-call(bf16[128,160]{1,0:T(8,128)(2,1)S(1)} %get-tuple-element.7.hub_ref, bf16[160,81920]{1,0:T(8,128)(2,1)S(1)} %get-tuple-element.8.all_ref), custom_call_target="tpu_custom_call" | custom-call | tf_op jit(solution)/shard_map/apply_potential/pallas_call | solution.py:454
